TPU v7x, 32 devices: a whole 2x2x4 slice. The times are simulated.
32 devices in a mesh: groups: 2 (over y), rows: 4 (over z), sub: 4 (over x, core).
Axes of the slice: x: 2, y: 2, z: 4, core: 2. Of those that a mesh axis runs over, the one named last changes fastest.
Arguments:
- matrix: float32 [16384, 1024], P(('groups', 'rows', 'sub')), parts along dimension 0
- sign_bits: int32 [16384], P(('groups', 'rows', 'sub')), parts along dimension 0, may hold values from 0 to 1
- samples: int32 [8192], P('groups'), parts along dimension 0, may hold values from 0 to 8191
Outputs:
- cholesky_factor: float32 [2048, 1024], P('groups'), parts along dimension 0
There are 2 independent parts, one for each index of `groups`. A program takes and returns all parts, laid end to end along the dimension named above; each array names one. Nothing has to cross between parts.
Inputs may be any that keep to these rules, and one draw needn't show every extreme that they name: `samples`: row numbers of the whole matrix, drawn independently; a row may be drawn more than once.
All inputs are finite; a program needn't handle non-finite values.
Results may differ from a plain program's by a relative error of at most 0.00011.
Values sent between devices are 32-bit elements; how exact they have to be, the bound alone decides.
No kernel may reach another device: no remote copies, remote signals or barrier semaphores. Data moves between devices by JAX's collectives and lax.ppermute only.
A program may use at most 64 MiB of HBM per device.

v0:
```python
import jax
import jax.numpy as jnp
from jax import lax
from jax.sharding import PartitionSpec as P

HIGHEST = lax.Precision.HIGHEST


def hadamard_table(extent):
    line_ids = jnp.arange(extent, dtype=jnp.int32)
    correlation = jnp.bitwise_and(line_ids[:, None], line_ids[None, :])
    parity = jnp.zeros((extent, extent), jnp.int32)
    for bit_pos in range(extent.bit_length() - 1):
        parity = parity + jnp.bitwise_and(jnp.right_shift(correlation, bit_pos), 1)
    return (1 - 2 * (parity % 2)).astype(jnp.float32)


def local_transform(values):
    rows_here, columns = values.shape
    inner_size = min(rows_here, 128)
    outer_size = rows_here // inner_size
    blocks = values.reshape(outer_size, inner_size, columns)
    blocks = jnp.einsum("ab,qbn->qan", hadamard_table(inner_size), blocks, precision=HIGHEST)
    blocks = jnp.einsum("pq,qan->pan", hadamard_table(outer_size), blocks, precision=HIGHEST)
    return blocks.reshape(rows_here, columns)


def mix_sources(received):
    return jnp.einsum("ab,bjn->ajn", hadamard_table(received.shape[0]), received, precision=HIGHEST)


def body(matrix, sign_bits, samples):
    rows_here, columns = matrix.shape
    devices = lax.axis_size(("rows", "sub"))
    position = lax.axis_index(("rows", "sub"))
    per_block = rows_here // devices
    sign_values = (2 * sign_bits - 1).astype(jnp.float32)
    current = local_transform(matrix * sign_values[:, None])
    block_ids = (
        (jnp.arange(devices, dtype=jnp.int32) * rows_here)[:, None]
        + position * per_block
        + jnp.arange(per_block, dtype=jnp.int32)[None, :]
    )
    blocks = current.reshape(devices, per_block, columns)
    mixed_rows = mix_sources(
        lax.all_to_all(blocks, ("rows", "sub"), split_axis=0, concat_axis=0, tiled=True)
    )
    owned_rows = mixed_rows.reshape(rows_here, columns)
    row_ids = block_ids.reshape(rows_here)
    matches = (row_ids[:, None] == samples[None, :]).astype(jnp.float32)
    counts = jnp.sum(matches, axis=1)
    weighted = owned_rows * counts[:, None]
    total_rows = rows_here * devices
    own_terms = jnp.einsum("rn,rm->nm", weighted, owned_rows, precision=HIGHEST) / jnp.float32(
        total_rows * samples.shape[0]
    )
    gram_matrix = lax.psum(own_terms, ("rows", "sub"))
    return jnp.linalg.cholesky(gram_matrix)


def solution(mesh):
    placed = (P(("groups", "rows", "sub"), None), P(("groups", "rows", "sub")), P("groups"))
    return jax.shard_map(
        body, mesh=mesh, in_specs=placed, out_specs=P("groups", None), check_vma=False
    )
```

profile of v0, /device:TPU:0, one launch (start us, length us, event | category | flops | bytes accessed | tf_op | source)
XLA Modules:
  0.0 427.4 jit_solution(5437568680601087725)
XLA Ops:
  6.5 0.7 add_convert_fusion
  7.2 1.8 broadcast_multiply_fusion
  9.0 3.5 convolution_bitcast_fusion
  12.5 2.0 copy.23
  14.5 5.4 %fusion.69 = f32[4,128,1024]{2,0,1:T(4,128)S(1)} fusion(f32[4,128,1024]{2,0,1:T(4,128)} %copy.23), kind=kOutput, calls=%fused_computation.112 | convolution fusion | flops 25166144 | bytes 4194304 | tf_op jit(solution)/shard_map/pq,qan->pan/dot_general | solution.py:24
  19.9 2.5 copy.24
  22.4 7.4 %all-to-all-start = ((f32[16,32,1024]{2,1,0:T(8,128)}), f32[16,32,1024]{2,1,0:T(8,128)S(1)}, u32[]{:S(2)}, u32[]{:S(2)}) async-start(f32[16,32,1024]{2,1,0:T(8,128)} %bitcast.60), calls=%async_computation | async-start | bytes 4194304 | tf_op jit(solution)/shard_map/all_to_all | solution.py:46
  29.8 0.2 all-reduce.3.cloned.1.call-start
  30.1 0.1 add.178
  30.2 1.0 convert_reduce_fusion
  31.2 0.1 mul.57
  31.3 0.1 copy.26
  31.4 39.4 %all-to-all-done = f32[16,32,1024]{2,1,0:T(8,128)S(1)} async-done(((f32[16,32,1024]{2,1,0:T(8,128)}), f32[16,32,1024]{2,1,0:T(8,128)S(1)}, u32[]{:S(2)}, u32[]{:S(2)}) %all-to-all-start) | async-done | bytes 2097184 | tf_op jit(solution)/shard_map/all_to_all | solution.py:46
  70.8 2.9 fusion.5
  73.7 8.9 %bitcast_multiply_fusion = f32[1024,1024]{0,1:T(8,128)} fusion(f32[16,32,1024]{2,0,1:T(8,128)S(1)} %fusion.5, f32[16,32]{0,1:T(8,128)S(1)} %copy.26), kind=kOutput, calls=%fused_computation.3 | convolution fusion | flops 6444023808 | bytes 6293504 | tf_op jit(solution)/shard_map/rn,rm->nm/dot_general | solution.py:54
  82.6 117.7 %all-reduce.3.cloned.1.call-done = f32[1024,1024]{0,1:T(8,128)} async-done(((f32[1024,1024]{0,1:T(8,128)}), f32[1024,1024]{0,1:T(8,128)}) %all-reduce.3.cloned.1.call-update) | async-done | bytes 4194320 | tf_op jit(solution)/shard_map/psum | solution.py:57
  200.3 5.5 %copy.28 = f32[1024,1024]{1,0:T(8,128)} copy(f32[1024,1024]{0,1:T(8,128)} %all-reduce.3.cloned.1.call-done) | data formatting | bytes 8388608 | tf_op jit(solution)/shard_map/psum | solution.py:57
  205.8 4.4 %fusion = f32[1024,1024]{1,0:T(8,128)S(1)} fusion(f32[1024,1024]{1,0:T(8,128)} %copy.28, f32[1024,1024]{0,1:T(8,128)} %all-reduce.3.cloned.1.call-done), kind=kLoop, calls=%fused_computation.2 | loop fusion | flops 2097152 | bytes 12582912 | tf_op jit(solution)/shard_map/jit(cholesky)/div | solution.py:58
  210.3 1.9 copy-done
  212.2 11.7 %cholesky.223 = f32[128,128]{1,0:T(8,128)S(1)} custom-call(f32[128,128]{1,0:T(8,128)S(1)} %cholesky.580), custom_call_target="Cholesky" | custom-call | tf_op jit(solution)/shard_map/jit(cholesky)/cholesky | solution.py:58
  224.0 9.8 %custom-call.59 = f32[1,128,128]{1,2,0:T(8,128)S(1)} custom-call(f32[1,128,128]{2,1,0:T(8,128)S(1)} %get-tuple-element.26), custom_call_target="InvertDiagBlocksLowerTriangular" | custom-call | tf_op jit(solution)/shard_map/jit(cholesky)/cholesky | solution.py:58
  233.8 2.5 cholesky.255
  236.3 2.3 constant_dynamic-update-slice_fusion.5
  238.6 1.5 convolution_subtract_fusion
  240.2 12.1 %cholesky.244 = f32[128,128]{1,0:T(8,128)S(1)} custom-call(f32[128,128]{1,0:T(8,128)S(1)} %cholesky.584), custom_call_target="Cholesky" | custom-call | tf_op jit(solution)/shard_map/jit(cholesky)/cholesky | solution.py:58
  252.3 0.6 select_reduce_fusion.6
  252.9 9.8 %custom-call.60 = f32[1,128,128]{1,2,0:T(8,128)S(1)} custom-call(f32[1,128,128]{2,1,0:T(8,128)S(1)} %get-tuple-element.23), custom_call_target="InvertDiagBlocksLowerTriangular" | custom-call | tf_op jit(solution)/shard_map/jit(cholesky)/cholesky | solution.py:58
  262.7 1.2 convolution_dynamic-update-slice_fusion
  263.9 2.1 convolution_subtract_fusion.1
  266.1 11.7 %cholesky.468 = f32[128,128]{1,0:T(8,128)S(1)} custom-call(f32[128,128]{1,0:T(8,128)S(1)} %cholesky.589), custom_call_target="Cholesky" | custom-call | tf_op jit(solution)/shard_map/jit(cholesky)/cholesky | solution.py:58
  277.8 0.6 select_reduce_fusion.5
  278.4 0.6 compare_reduce_fusion.5
  279.1 9.8 %custom-call.61 = f32[1,128,128]{1,2,0:T(8,128)S(1)} custom-call(f32[1,128,128]{2,1,0:T(8,128)S(1)} %get-tuple-element.20), custom_call_target="InvertDiagBlocksLowerTriangular" | custom-call | tf_op jit(solution)/shard_map/jit(cholesky)/cholesky | solution.py:58
  288.9 1.1 convolution_dynamic-update-slice_fusion.1
  290.0 2.3 convolution_subtract_fusion.2
  292.4 11.8 %cholesky.487 = f32[128,128]{1,0:T(8,128)S(1)} custom-call(f32[128,128]{1,0:T(8,128)S(1)} %cholesky.594), custom_call_target="Cholesky" | custom-call | tf_op jit(solution)/shard_map/jit(cholesky)/cholesky | solution.py:58
  304.2 0.6 select_reduce_fusion.4
  304.9 0.7 compare_reduce_fusion.4
  305.5 9.8 %custom-call.62 = f32[1,128,128]{1,2,0:T(8,128)S(1)} custom-call(f32[1,128,128]{2,1,0:T(8,128)S(1)} %get-tuple-element.17), custom_call_target="InvertDiagBlocksLowerTriangular" | custom-call | tf_op jit(solution)/shard_map/jit(cholesky)/cholesky | solution.py:58
  315.3 1.1 convolution_dynamic-update-slice_fusion.2
  316.4 2.3 convolution_subtract_fusion.3
  318.8 11.7 %cholesky.506 = f32[128,128]{1,0:T(8,128)S(1)} custom-call(f32[128,128]{1,0:T(8,128)S(1)} %cholesky.599), custom_call_target="Cholesky" | custom-call | tf_op jit(solution)/shard_map/jit(cholesky)/cholesky | solution.py:58
  330.5 0.6 select_reduce_fusion.3
  331.1 0.7 compare_reduce_fusion.3
  331.8 10.0 %custom-call.63 = f32[1,128,128]{1,2,0:T(8,128)S(1)} custom-call(f32[1,128,128]{2,1,0:T(8,128)S(1)} %get-tuple-element.14), custom_call_target="InvertDiagBlocksLowerTriangular" | custom-call | tf_op jit(solution)/shard_map/jit(cholesky)/cholesky | solution.py:58
  341.8 1.0 convolution_dynamic-update-slice_fusion.3
  342.8 2.3 convolution_subtract_fusion.4
  345.1 11.7 %cholesky.526 = f32[128,128]{1,0:T(8,128)S(1)} custom-call(f32[128,128]{1,0:T(8,128)S(1)} %cholesky.604), custom_call_target="Cholesky" | custom-call | tf_op jit(solution)/shard_map/jit(cholesky)/cholesky | solution.py:58
  356.8 0.6 select_reduce_fusion.2
  357.5 0.6 compare_reduce_fusion.2
  358.1 9.8 %custom-call.64 = f32[1,128,128]{1,2,0:T(8,128)S(1)} custom-call(f32[1,128,128]{2,1,0:T(8,128)S(1)} %get-tuple-element.11), custom_call_target="InvertDiagBlocksLowerTriangular" | custom-call | tf_op jit(solution)/shard_map/jit(cholesky)/cholesky | solution.py:58
  367.9 0.9 convolution_dynamic-update-slice_fusion.4
  368.8 2.1 convolution_subtract_fusion.5
  371.0 11.9 %cholesky.546 = f32[128,128]{1,0:T(8,128)S(1)} custom-call(f32[128,128]{1,0:T(8,128)S(1)} %cholesky.609), custom_call_target="Cholesky" | custom-call | tf_op jit(solution)/shard_map/jit(cholesky)/cholesky | solution.py:58
  382.9 0.6 select_reduce_fusion.1
  383.5 0.6 compare_reduce_fusion.1
  384.2 9.8 %custom-call.65 = f32[1,128,128]{1,2,0:T(8,128)S(1)} custom-call(f32[1,128,128]{2,1,0:T(8,128)S(1)} %get-tuple-element.8), custom_call_target="InvertDiagBlocksLowerTriangular" | custom-call | tf_op jit(solution)/shard_map/jit(cholesky)/cholesky | solution.py:58
  394.0 0.8 convolution_dynamic-update-slice_fusion.5
  394.8 1.8 convolution_subtract_fusion.6
  396.6 11.7 %cholesky.564 = f32[128,128]{1,0:T(8,128)S(1)} custom-call(f32[128,128]{1,0:T(8,128)S(1)} %convolution_subtract_fusion.6), custom_call_target="Cholesky" | custom-call | tf_op jit(solution)/shard_map/jit(cholesky)/cholesky | solution.py:58
  408.3 0.6 select_reduce_fusion
  409.0 0.7 compare_reduce_fusion
  409.7 0.7 compare_reduce_fusion.6
  415.3 4.9 %select_select_fusion = f32[1024,1024]{1,0:T(8,128)} fusion(f32[1024,1024]{1,0:T(8,128)} %get-tuple-element.6, pred[]{:T(512)S(6)} %cholesky.579), kind=kLoop, calls=%fused_computation.4 | loop fusion | flops 3145728 | bytes 8388609 | tf_op jit(solution)/shard_map/jit(cholesky)/select_n | solution.py:58
  (14 shorter events, 0.2 us)
Async XLA Ops:
  19.9 10.3 %copy-start.1 = (s32[4096]{0:T(1024)S(1)}, s32[4096]{0:T(1024)}, u32[]{:S(2)}) copy-start(s32[4096]{0:T(1024)} %param.5) | copy-start | bytes 49156
  22.4 48.4 %all-to-all-start = ((f32[16,32,1024]{2,1,0:T(8,128)}), f32[16,32,1024]{2,1,0:T(8,128)S(1)}, u32[]{:S(2)}, u32[]{:S(2)}) async-start(f32[16,32,1024]{2,1,0:T(8,128)} %bitcast.60), calls=%async_computation | async-start | bytes 4194304 | tf_op jit(solution)/shard_map/all_to_all | solution.py:46
  29.8 170.5 %all-reduce.3.cloned.1.call-start = ((), (), s32[]{:S(2)}) async-start(), calls=%async_computation.1 | async-start | bytes 8388608 | tf_op jit(solution)/shard_map/psum | solution.py:57
  210.3 1.9 copy-start
Sparse Core Ops, SparseCore 0:
  82.7 117.5 all-reduce.2
where the time goes:
time: 435 us; the launch traced here: 427 us
  other arithmetic  185 us (43%)
  waiting for transfers between devices  157 us (36%)
  matrix products  43.6 us (10%)
  between operations  19 us (4%)
  local copies, waits for them, and re-layouts  14.8 us (3%)
  starting transfers between devices  7.6 us (2%)
    another operation x30, other arithmetic, body(): return jnp.linalg.cholesky(gram_matrix)  172 us
    psum x1, waiting for transfers between devices, body(): gram_matrix = lax.psum(own_terms, ('rows', 'sub'))  118 us
    all_to_all x1, waiting for transfers between devices, body(): lax.all_to_all(blocks, ('rows', 'sub'), split_axis=0, concat_axis=0, tile...  39.4 us
    another operation x14, matrix products, body(): return jnp.linalg.cholesky(gram_matrix)  22.9 us
    dot_general x1, matrix products, body(): jnp.einsum('rn,rm->nm', weighted, owned_rows, precision=HIGHEST)  8.89 us
  transfers between devices with their start and end apart: 2, of which 2 were waited for; matrix products, arithmetic and copies ran while one was open for 0% of the time, Pallas kernels for 0%

commit v1 on v0

--- a/solution.py
+++ b/solution.py
@@ -1,9 +1,13 @@
 import jax
 import jax.numpy as jnp
 from jax import lax
+from jax.experimental import pallas as pl
+from jax.experimental.pallas import tpu as pltpu
 from jax.sharding import PartitionSpec as P
 
 HIGHEST = lax.Precision.HIGHEST
+BLOCK = 128
+GROUP = 8
 
 
 def hadamard_table(extent):
@@ -29,6 +33,117 @@
     return jnp.einsum("ab,bjn->ajn", hadamard_table(received.shape[0]), received, precision=HIGHEST)
 
 
+def factor_block(block):
+    sub_ids = lax.broadcasted_iota(jnp.int32, (GROUP, BLOCK), 0)
+    lane_ids = lax.broadcasted_iota(jnp.int32, (GROUP, BLOCK), 1)
+    count = BLOCK // GROUP
+    rows = [block[GROUP * t : GROUP * (t + 1), :] for t in range(count)]
+    extra = [jnp.where(lane_ids == sub_ids + GROUP * t, 1.0, 0.0).astype(jnp.float32) for t in range(count)]
+    upper, inverse = [], []
+
+    def spread(value, index):
+        return jnp.broadcast_to(value[index : index + 1, :], (GROUP, BLOCK))
+
+    for g in range(count):
+        own, aug = rows[g], extra[g]
+        cols = [jnp.broadcast_to(own[:, GROUP * g + j : GROUP * g + j + 1], (GROUP, BLOCK)) for j in range(GROUP)]
+        own_out, aug_out = own, aug
+        for j in range(GROUP):
+            factor = cols[j]
+            pivot = spread(factor, j)
+            root = lax.rsqrt(pivot)
+            here = sub_ids == j
+            own_row, aug_row = spread(own, j) * root, spread(aug, j) * root
+            own_out = jnp.where(here, own_row, own_out)
+            aug_out = jnp.where(here, aug_row, aug_out)
+            multiplier = jnp.where(here, -root, factor * root)
+            own = jnp.where(here, 0.0, own) - multiplier * own_row
+            aug = jnp.where(here, 0.0, aug) - multiplier * aug_row
+            for m in range(j + 1, GROUP):
+                line = spread(cols[m], j) * root
+                cols[m] = jnp.where(here, 0.0, cols[m]) - multiplier * line
+        upper.append(jnp.where(lane_ids >= sub_ids + GROUP * g, own_out, 0.0))
+        inverse.append(aug_out)
+        own_lines = [spread(own, j) for j in range(GROUP)]
+        aug_lines = [spread(aug, j) for j in range(GROUP)]
+        for t in range(g + 1, count):
+            source = rows[t]
+            own_sum = aug_sum = None
+            for j in range(GROUP):
+                column = jnp.broadcast_to(source[:, GROUP * g + j : GROUP * g + j + 1], (GROUP, BLOCK))
+                own_term, aug_term = column * own_lines[j], column * aug_lines[j]
+                own_sum = own_term if own_sum is None else own_sum + own_term
+                aug_sum = aug_term if aug_sum is None else aug_sum + aug_term
+            rows[t] = source - own_sum
+            extra[t] = extra[t] - aug_sum
+    return jnp.concatenate(upper, axis=0), jnp.concatenate(inverse, axis=0)
+
+
+def transposed_dot(left, right):
+    return lax.dot_general(
+        left, right, (((0,), (0,)), ((), ())), precision=HIGHEST, preferred_element_type=jnp.float32
+    )
+
+
+def panel_kernel(offset, columns, last, *refs):
+    gram_ref, *earlier = refs[: -2 if last else -1]
+    out_ref = refs[-2] if last else refs[-1]
+    own_ref = refs[-1]
+    height, width = gram_ref.shape
+    current = gram_ref[...]
+    for ref in earlier:
+        skip = ref.shape[1] - width
+        current = current - transposed_dot(ref[:, skip : skip + height], ref[:, skip:])
+    own_ref[...] = current
+    steps = height // BLOCK
+
+    def step(k):
+        base = BLOCK * k
+        upper, inverse = factor_block(own_ref[base : base + BLOCK, base : base + BLOCK])
+        own_ref[base : base + BLOCK, base : base + BLOCK] = upper
+        right = base + BLOCK
+        if right < width:
+            solved = jnp.dot(
+                inverse, own_ref[base : base + BLOCK, right:], precision=HIGHEST, preferred_element_type=jnp.float32
+            )
+            own_ref[base : base + BLOCK, right:] = solved
+            if right < height:
+                own_ref[right:, right:] = own_ref[right:, right:] - transposed_dot(
+                    solved[:, : height - right], solved
+                )
+        if base:
+            own_ref[base : base + BLOCK, :base] = jnp.zeros((BLOCK, base), jnp.float32)
+
+    for k in range(steps):
+        step(k)
+    if last:
+        out_ref[...] = jnp.zeros((columns, columns), jnp.float32)
+        for ref in [*earlier, own_ref]:
+            tall, wide = ref.shape
+            start = columns - wide
+            out_ref[start:, start : start + tall] = ref[...].T
+
+
+def factor_panel(gram_rows, earlier, columns):
+    height, width = gram_rows.shape
+    last = height == width
+    args = 1 + len(earlier)
+    scratch = [pltpu.VMEM((height, width), jnp.float32)] if last else []
+    shape = (columns, columns) if last else (height, width)
+
+    def kernel(*refs):
+        panel_kernel(columns - width, columns, last, *refs)
+
+    return pl.pallas_call(
+        kernel,
+        out_shape=jax.ShapeDtypeStruct(shape, jnp.float32),
+        in_specs=[pl.BlockSpec(memory_space=pltpu.VMEM)] * args,
+        out_specs=pl.BlockSpec(memory_space=pltpu.VMEM),
+        scratch_shapes=scratch,
+        compiler_params=pltpu.CompilerParams(vmem_limit_bytes=48 * 1024 * 1024),
+    )(gram_rows, *earlier)
+
+
 def body(matrix, sign_bits, samples):
     rows_here, columns = matrix.shape
     devices = lax.axis_size(("rows", "sub"))
@@ -48,14 +163,21 @@
     owned_rows = mixed_rows.reshape(rows_here, columns)
     row_ids = block_ids.reshape(rows_here)
     matches = (row_ids[:, None] == samples[None, :]).astype(jnp.float32)
-    counts = jnp.sum(matches, axis=1)
+    counts = jnp.sum(matches, axis=1) / jnp.float32(rows_here * devices * samples.shape[0])
     weighted = owned_rows * counts[:, None]
-    total_rows = rows_here * devices
-    own_terms = jnp.einsum("rn,rm->nm", weighted, owned_rows, precision=HIGHEST) / jnp.float32(
-        total_rows * samples.shape[0]
-    )
-    gram_matrix = lax.psum(own_terms, ("rows", "sub"))
-    return jnp.linalg.cholesky(gram_matrix)
+    height = columns // 4
+    summed = []
+    for start in range(0, columns, height):
+        own = jnp.einsum(
+            "rn,rm->nm", weighted[:, start : start + height], owned_rows[:, start:], precision=HIGHEST
+        )
+        if summed:
+            own, summed[-1] = lax.optimization_barrier((own, summed[-1]))
+        summed.append(lax.psum(own, ("rows", "sub")))
+    panels = []
+    for gram_rows in summed:
+        panels.append(factor_panel(gram_rows, panels, columns))
+    return panels[-1]
 
 
 def solution(mesh):

time: 435 us -> 489 us (1.12)
  waiting for transfers between devices: 157 us -> 379 us
  other arithmetic: 185 us -> 3.77 us
  Pallas kernels: 0 us -> 44.8 us
  matrix products: 43.6 us -> 24 us
  local copies, waits for them, and re-layouts: 14.8 us -> 8.27 us
  between operations: 19 us -> 13.7 us
    psum x1 -> x4, waiting for transfers between devices: 118 us -> 339 us  [body(): summed.append(lax.psum(own, ('rows', 'sub')))]
    another operation x30 -> x0, other arithmetic: 172 us -> none  [body(): return jnp.linalg.cholesky(gram_matrix)]
    pallas_call x0 -> x4, Pallas kernels: none -> 44.8 us  [factor_panel(): pl.pallas_call(kernel, out_shape=jax.ShapeDtypeStruct(shape, jnp.float32)...]
    another operation x14 -> x0, matrix products: 22.9 us -> none  [body(): return jnp.linalg.cholesky(gram_matrix)]
    psum x1 -> x0, local copies, waits for them, and re-layouts: 5.53 us -> none  [body(): gram_matrix = lax.psum(own_terms, ('rows', 'sub'))]
    dot_general x1 -> x4, matrix products: 8.89 us -> 12.3 us  [body(): jnp.einsum('rn,rm->nm', weighted[:, start:start + height], owned_rows[:,...]
  transfers between devices with their start and end apart: 2 -> 5, of which waited for: 2 -> 5; matrix products, arithmetic and copies ran while one was open for 0% -> 2% of each run, Pallas kernels for 0% -> 7%
where the time goes in v1:
time: 489 us; the launch traced here: 482 us
  waiting for transfers between devices  379 us (78%)
  Pallas kernels  44.8 us (9%)
  matrix products  24 us (5%)
  between operations  13.7 us (3%)
  starting transfers between devices  8.31 us (2%)
  local copies, waits for them, and re-layouts  8.27 us (2%)
    psum x4, waiting for transfers between devices, body(): summed.append(lax.psum(own, ('rows', 'sub')))  339 us
    pallas_call x4, Pallas kernels, factor_panel(): pl.pallas_call(kernel, out_shape=jax.ShapeDtypeStruct(shape, jnp.float32)...  44.8 us
    all_to_all x1, waiting for transfers between devices, body(): lax.all_to_all(blocks, ('rows', 'sub'), split_axis=0, concat_axis=0, tile...  39.3 us
    dot_general x4, matrix products, body(): jnp.einsum('rn,rm->nm', weighted[:, start:start + height], owned_rows[:,...  12.3 us
  transfers between devices with their start and end apart: 5, of which 5 were waited for; matrix products, arithmetic and copies ran while one was open for 2% of the time, Pallas kernels for 7%

profile of v1, /device:TPU:0, one launch (start us, length us, event | category | flops | bytes accessed | tf_op | source)
XLA Modules:
  0.0 481.6 jit_solution(2488500610702703181)
XLA Ops:
  6.5 0.7 add_convert_fusion
  7.2 1.8 broadcast_multiply_fusion.1
  9.0 3.5 convolution_bitcast_fusion
  12.5 2.0 copy.13
  14.5 5.4 %fusion.47 = f32[4,128,1024]{2,0,1:T(4,128)S(1)} fusion(f32[4,128,1024]{2,0,1:T(4,128)} %copy.13), kind=kOutput, calls=%fused_computation.59 | convolution fusion | flops 25166144 | bytes 4194304 | tf_op jit(solution)/shard_map/pq,qan->pan/dot_general | solution.py:28
  19.9 2.5 copy.14
  22.4 0.0 copy-start.6
  22.4 7.5 %all-to-all-start = ((f32[16,32,1024]{2,1,0:T(8,128)}), f32[16,32,1024]{2,1,0:T(8,128)S(1)}, u32[]{:S(2)}, u32[]{:S(2)}) async-start(f32[16,32,1024]{2,1,0:T(8,128)} %bitcast.22), calls=%async_computation | async-start | bytes 4194304 | tf_op jit(solution)/shard_map/all_to_all | solution.py:161
  29.9 0.5 all-reduce.5.cloned.1.call-start
  30.5 0.1 iota_add_fusion
  30.5 0.1 add.110
  30.6 0.0 copy-done.6
  30.6 1.0 convert_reduce_fusion
  31.6 39.3 %all-to-all-done = f32[16,32,1024]{2,1,0:T(8,128)S(1)} async-done(((f32[16,32,1024]{2,1,0:T(8,128)}), f32[16,32,1024]{2,1,0:T(8,128)S(1)}, u32[]{:S(2)}, u32[]{:S(2)}) %all-to-all-start) | async-done | bytes 2097184 | tf_op jit(solution)/shard_map/all_to_all | solution.py:161
  70.9 2.8 fusion
  73.8 1.2 copy.16
  75.0 0.0 copy-start.4
  75.0 0.2 broadcast_multiply_fusion
  75.2 0.0 copy-start.5
  75.2 1.5 copy-done.5
  76.7 2.9 fusion.6
  79.6 0.0 all-reduce.5.cloned.1.call-update
  79.6 0.0 all-reduce.7.cloned.1.call-start
  79.7 3.4 fusion.2
  83.1 97.0 %all-reduce.5.cloned.1.call-done.refs_0_ = f32[256,1024]{1,0:T(8,128)} async-done(((f32[256,1024]{1,0:T(8,128)}), f32[256,1024]{1,0:T(8,128)}) %all-reduce.5.cloned.1.call-update) | async-done | bytes 1048592 | tf_op jit(solution)/shard_map/psum | solution.py:176
  180.2 0.0 all-reduce.7.cloned.1.call-update
  180.2 0.0 copy-start
  180.2 0.0 all-reduce.9.cloned.1.call-start
  180.3 0.0 copy-done.4
  180.3 3.0 fusion.4
  183.2 92.1 %all-reduce.7.cloned.1.call-done.refs_0_ = f32[256,768]{1,0:T(8,128)} async-done(((f32[256,768]{1,0:T(8,128)}), f32[256,768]{1,0:T(8,128)}) %all-reduce.7.cloned.1.call-update) | async-done | bytes 786448 | tf_op jit(solution)/shard_map/psum | solution.py:176
  275.3 0.0 copy-start.1
  275.3 0.0 all-reduce.9.cloned.1.call-update
  275.4 0.2 all-reduce.11.cloned.1.call-start
  275.6 2.9 fusion.10
  278.5 90.0 %all-reduce.9.cloned.1.call-done.refs_0_ = f32[256,512]{1,0:T(8,128)} async-done(((f32[256,512]{1,0:T(8,128)}), f32[256,512]{1,0:T(8,128)}) %all-reduce.9.cloned.1.call-update) | async-done | bytes 524304 | tf_op jit(solution)/shard_map/psum | solution.py:176
  368.5 0.0 all-reduce.11.cloned.1.call-update
  368.6 0.0 copy-done
  368.6 0.0 copy-start.2
  368.6 10.7 %shard_map.37.refs_1_ = f32[256,1024]{1,0:T(8,128)S(1)} custom-call(f32[256,1024]{1,0:T(8,128)S(1)} %copy-done), custom_call_target="tpu_custom_call" | custom-call | tf_op jit(solution)/shard_map/pallas_call | solution.py:137
  379.3 0.0 copy-done.1
  379.3 11.2 %shard_map.38.refs_2_ = f32[256,768]{1,0:T(8,128)S(1)} custom-call(f32[256,768]{1,0:T(8,128)S(1)} %copy-done.1, f32[256,1024]{1,0:T(8,128)S(1)} %shard_map.37.refs_1_), custom_call_target="tpu_custom_call" | custom-call | tf_op jit(solution)/shard_map/pallas_call | solution.py:137
  390.5 0.0 copy-done.2
  390.5 11.2 %shard_map.39.refs_3_ = f32[256,512]{1,0:T(8,128)S(1)} custom-call(f32[256,512]{1,0:T(8,128)S(1)} %copy-done.2, f32[256,1024]{1,0:T(8,128)S(1)} %shard_map.37.refs_1_, f32[256,768]{1,0:T(8,128)S(1)} %shard_map.38.refs_2_), custom_call_target="tpu_custom_call" | custom-call | tf_op jit(solution)/shard_map/pallas_call | solution.py:137
  401.8 60.3 %all-reduce.11.cloned.1.call-done.refs_0_ = f32[256,256]{1,0:T(8,128)} async-done(((f32[256,256]{1,0:T(8,128)}), f32[256,256]{1,0:T(8,128)}) %all-reduce.11.cloned.1.call-update) | async-done | bytes 262160 | tf_op jit(solution)/shard_map/psum | solution.py:176
  462.1 0.0 copy-start.3
  462.1 0.9 copy-done.3
  463.0 11.6 %shard_map.40 = f32[1024,1024]{1,0:T(8,128)} custom-call(f32[256,256]{1,0:T(8,128)S(1)} %copy-done.3, f32[256,1024]{1,0:T(8,128)S(1)} %shard_map.37.refs_1_, f32[256,768]{1,0:T(8,128)S(1)} %shard_map.38.refs_2_, f32[256,512]{1,0:T(8,128)S(1)} %shard_map.39.refs_3_), custom_call_target="tpu_custom_call" | custom-call | tf_op jit(solution)/shard_map/pallas_call | solution.py:137
  (2 shorter events, 0.0 us)
Async XLA Ops:
  22.4 8.2 %copy-start.6 = (s32[4096]{0:T(1024)S(1)}, s32[4096]{0:T(1024)}, u32[]{:S(2)}) copy-start(s32[4096]{0:T(1024)} %param.5) | copy-start | bytes 49156
  22.4 48.5 %all-to-all-start = ((f32[16,32,1024]{2,1,0:T(8,128)}), f32[16,32,1024]{2,1,0:T(8,128)S(1)}, u32[]{:S(2)}, u32[]{:S(2)}) async-start(f32[16,32,1024]{2,1,0:T(8,128)} %bitcast.22), calls=%async_computation | async-start | bytes 4194304 | tf_op jit(solution)/shard_map/all_to_all | solution.py:161
  29.9 150.2 %all-reduce.5.cloned.1.call-start = ((), (), s32[]{:S(2)}) async-start(), calls=%async_computation.1 | async-start | bytes 2097152 | tf_op jit(solution)/shard_map/psum | solution.py:176
  75.0 105.3 %copy-start.4 = (f32[16,32,1024]{2,1,0:T(8,128)}, f32[16,32,1024]{2,1,0:T(8,128)S(1)}, u32[]{:S(2)}) copy-start(f32[16,32,1024]{2,1,0:T(8,128)S(1)} %copy.16) | copy-start | bytes 6291460
  75.2 1.5 copy-start.5
  79.6 195.7 %all-reduce.7.cloned.1.call-start = ((), (), s32[]{:S(2)}) async-start(), calls=%async_computation.2 | async-start | bytes 1572864 | tf_op jit(solution)/shard_map/psum | solution.py:176
  180.2 188.4 %copy-start = (f32[256,1024]{1,0:T(8,128)S(1)}, f32[256,1024]{1,0:T(8,128)}, u32[]{:S(2)}) copy-start(f32[256,1024]{1,0:T(8,128)} %all-reduce.5.cloned.1.call-done.refs_0_) | copy-start | bytes 3145732
  180.2 188.3 %all-reduce.9.cloned.1.call-start = ((), (), s32[]{:S(2)}) async-start(), calls=%async_computation.3 | async-start | bytes 1048576 | tf_op jit(solution)/shard_map/psum | solution.py:176
  275.3 104.0 %copy-start.1 = (f32[256,768]{1,0:T(8,128)S(1)}, f32[256,768]{1,0:T(8,128)}, u32[]{:S(2)}) copy-start(f32[256,768]{1,0:T(8,128)} %all-reduce.7.cloned.1.call-done.refs_0_) | copy-start | bytes 2359300
  275.4 186.7 %all-reduce.11.cloned.1.call-start = ((), (), s32[]{:S(2)}) async-start(), calls=%async_computation.4 | async-start | bytes 524288 | tf_op jit(solution)/shard_map/psum | solution.py:176
  368.6 22.0 %copy-start.2 = (f32[256,512]{1,0:T(8,128)S(1)}, f32[256,512]{1,0:T(8,128)}, u32[]{:S(2)}) copy-start(f32[256,512]{1,0:T(8,128)} %all-reduce.9.cloned.1.call-done.refs_0_) | copy-start | bytes 1572868
  462.1 0.9 copy-start.3
Sparse Core Ops, SparseCore 0:
  79.8 100.3 all-reduce.4
  183.6 91.7 all-reduce.6
  278.7 89.7 all-reduce.8
  371.8 90.2 all-reduce.10
